TPU v7x, 32 devices: a 4x4x1 block of a 4x4x8 slice. The times are simulated.
32 devices in a mesh: batch: 1 (over z), row: 4 (over y), col: 8 (over x, core).
Axes of the slice: x: 4, y: 4, z: 1, core: 2. Of those that a mesh axis runs over, the one named last changes fastest.
The devices are a block of a 4x4x8 slice.
Arguments:
- lower_mat: bfloat16 [6144, 6144], P('row', 'col')
- rhs_mat: bfloat16 [6144, 768], P('row', ('batch', 'col'))
Outputs:
- output: bfloat16 [6144, 768], P('row', ('batch', 'col'))
All inputs are finite; a program needn't handle non-finite values.
Results may differ from a plain program's by a relative error of at most 0.001.
Values are sent between devices in bfloat16 or wider.
A program may use at most 768 MiB of HBM per device.

v0:
```python
import jax
import jax.numpy as jnp
from jax import lax
from jax.sharding import PartitionSpec as P

BLOCK_SIZE = 256


def solution(mesh):
    grid_rows = mesh.shape["row"]
    grid_cols = mesh.shape["col"]

    def local_product(lower_loc, rhs_loc):
        rows_loc = lower_loc.shape[0]
        rhs_cols = rhs_loc.shape[1]
        row_blocks = rows_loc // BLOCK_SIZE
        col_blocks = lower_loc.shape[1] // BLOCK_SIZE
        gathered_rhs = lax.all_gather(rhs_loc, "row", axis=0)
        rhs_steps = gathered_rhs.reshape(grid_rows, row_blocks, BLOCK_SIZE, rhs_cols).transpose(1, 0, 2, 3).reshape(col_blocks, grid_cols * BLOCK_SIZE, rhs_cols)
        block_sum = jnp.zeros((rows_loc, rhs_cols), jnp.float32)
        for step in range(col_blocks):
            first_row = (step * grid_cols // grid_rows) * BLOCK_SIZE
            panel = lower_loc[first_row:, step * BLOCK_SIZE:(step + 1) * BLOCK_SIZE]
            panels = lax.all_gather(panel, "col", axis=1, tiled=True)
            update = jnp.dot(panels, rhs_steps[step], preferred_element_type=jnp.float32)
            block_sum = lax.dynamic_update_slice(block_sum, block_sum[first_row:] + update, (first_row, 0))
        return block_sum.astype(jnp.bfloat16)

    return jax.shard_map(local_product, mesh=mesh, in_specs=(P("row", "col"), P("row", ("batch", "col"))), out_specs=P("row", ("batch", "col")), check_vma=False)
```

profile of v0, /device:TPU:98, one launch (start us, length us, event | category | flops | bytes accessed | tf_op | source)
XLA Modules:
  0.0 147.5 jit_solution(18103778475597909067)
XLA Ops:
  6.5 0.0 all-gather.12.cloned.1.call-start
  6.6 0.7 all-gather.12.cloned.1.call-update
  7.3 0.1 all-gather.6.cloned.1.call-start
  7.4 2.1 %slice.28 = bf16[1536,256]{1,0:T(8,128)(2,1)} slice(bf16[1536,768]{1,0:T(8,128)(2,1)} %param.2), slice={[0:1536], [0:256]} | slice | bytes 1572864 | tf_op jit(solution)/shard_map/slice | solution.py:23
  9.4 0.1 all-gather.6.cloned.1.call-update
  9.5 0.1 all-gather.8.cloned.1.call-start
  9.6 1.9 %slice.31 = bf16[1024,256]{1,0:T(8,128)(2,1)} slice(bf16[1536,768]{1,0:T(8,128)(2,1)} %param.2), slice={[512:1536], [256:512]} | slice | bytes 1048576 | tf_op jit(solution)/shard_map/slice | solution.py:23
  11.5 0.1 all-gather.8.cloned.1.call-update
  11.5 0.1 all-gather.10.cloned.1.call-start
  11.6 1.7 %slice.34 = bf16[512,256]{1,0:T(8,128)(2,1)} slice(bf16[1536,768]{1,0:T(8,128)(2,1)} %param.2), slice={[1024:1536], [512:768]} | slice | bytes 524288 | tf_op jit(solution)/shard_map/slice | solution.py:23
  13.3 0.1 all-gather.10.cloned.1.call-update
  13.3 20.7 %all-gather.12.cloned.1.call-done = bf16[6144,96]{0,1:T(8,128)(2,1)} async-done(((bf16[1536,96]{0,1:T(8,128)(2,1)}), bf16[6144,96]{0,1:T(8,128)(2,1)}) %all-gather.12.cloned.1.call-update) | async-done | bytes 1179664 | tf_op jit(solution)/shard_map/all_gather | solution.py:18
  34.0 2.9 %reshape.10 = bf16[4,6,256,96]{2,1,0,3:T(8,128)(2,1)S(1)} reshape(bf16[6144,96]{0,1:T(8,128)(2,1)} %all-gather.12.cloned.1.call-done) | data formatting | bytes 2359296 | tf_op jit(solution)/shard_map/reshape | solution.py:19
  36.9 0.8 fusion.1
  37.7 0.2 copy.3
  37.9 0.3 squeeze.9
  38.2 0.2 copy.4
  38.3 0.3 squeeze.10
  38.6 0.2 copy.5
  38.8 0.3 squeeze.11
  39.1 38.1 %all-gather.6.cloned.1.call-done = bf16[1536,2048]{1,0:T(8,128)(2,1)} async-done(((bf16[1536,256]{1,0:T(8,128)(2,1)}), bf16[1536,2048]{1,0:T(8,128)(2,1)}) %all-gather.6.cloned.1.call-update) | async-done | bytes 6291472 | tf_op jit(solution)/shard_map/all_gather | solution.py:24
  77.1 4.8 %fusion.2 = f32[1536,96]{0,1:T(8,128)S(1)} fusion(bf16[1536,2048]{1,0:T(8,128)(2,1)} %all-gather.6.cloned.1.call-done, bf16[2048,96]{0,1:T(8,128)(2,1)S(1)} %squeeze.9), kind=kOutput, calls=%fused_computation.5 | convolution fusion | flops 603979776 | bytes 7274496 | tf_op jit(solution)/shard_map/dot_general | solution.py:25
  82.0 29.8 %all-gather.8.cloned.1.call-done = bf16[1024,2048]{1,0:T(8,128)(2,1)} async-done(((bf16[1024,256]{1,0:T(8,128)(2,1)}), bf16[1024,2048]{1,0:T(8,128)(2,1)}) %all-gather.8.cloned.1.call-update) | async-done | bytes 4194320 | tf_op jit(solution)/shard_map/all_gather | solution.py:24
  111.8 3.6 %convolution_add_fusion = f32[1024,96]{0,1:T(8,128)S(1)} fusion(bf16[1024,2048]{1,0:T(8,128)(2,1)} %all-gather.8.cloned.1.call-done, bf16[2048,96]{0,1:T(8,128)(2,1)S(1)} %squeeze.10, f32[1536,96]{0,1:T(8,128)S(1)} %fusion.2), kind=kOutput, calls=%fused_computation | convolution fusion | flops 402751488 | bytes 5373952 | tf_op jit(solution)/shard_map/dot_general | solution.py:25
  115.5 22.4 %all-gather.10.cloned.1.call-done = bf16[512,2048]{1,0:T(8,128)(2,1)} async-done(((bf16[512,256]{1,0:T(8,128)(2,1)}), bf16[512,2048]{1,0:T(8,128)(2,1)}) %all-gather.10.cloned.1.call-update) | async-done | bytes 2097168 | tf_op jit(solution)/shard_map/all_gather | solution.py:24
  137.9 2.4 %fusion = f32[1536,96]{0,1:T(8,128)S(1)} fusion(f32[1536,96]{0,1:T(8,128)S(1)} %constant_dynamic-update-slice_fusion, bf16[512,2048]{1,0:T(8,128)(2,1)} %all-gather.10.cloned.1.call-done, bf16[2048,96]{0,1:T(8,128)(2,1)S(1)} %squeeze.11, f32[1024,96]{0,1:T(8,128)S(1)} %convolution_add_fusion), kind=kOutput, calls=%fused_computation.2 | convolution fusion | flops 201375744 | bytes 2883584 | tf_op jit(solution)/shard_map/dot_general | solution.py:25
  140.2 0.7 convert_element_type.3
  (1 shorter events, 0.0 us)
Async XLA Ops:
  6.5 27.5 %all-gather.12.cloned.1.call-start = ((), (), s32[]{:S(2)}) async-start(), calls=%async_computation.3 | async-start | bytes 1474560 | tf_op jit(solution)/shard_map/all_gather | solution.py:18
  7.3 69.8 %all-gather.6.cloned.1.call-start = ((), (), s32[]{:S(2)}) async-start(), calls=%async_computation | async-start | bytes 7077888 | tf_op jit(solution)/shard_map/all_gather | solution.py:24
  9.5 102.3 %all-gather.8.cloned.1.call-start = ((), (), s32[]{:S(2)}) async-start(), calls=%async_computation.1 | async-start | bytes 4718592 | tf_op jit(solution)/shard_map/all_gather | solution.py:24
  11.5 126.3 %all-gather.10.cloned.1.call-start = ((), (), s32[]{:S(2)}) async-start(), calls=%async_computation.2 | async-start | bytes 2359296 | tf_op jit(solution)/shard_map/all_gather | solution.py:24
Sparse Core Ops, SparseCore 0:
  8.9 25.0 all-gather.11
  35.6 41.5 all-gather.5
  78.7 33.0 all-gather.7
  113.3 24.5 all-gather.9
where the time goes:
time: 150 us; the launch traced here: 148 us
  waiting for transfers between devices  112 us (75%)
  between operations  13.2 us (9%)
  matrix products  10.8 us (7%)
  local copies, waits for them, and re-layouts  10.7 us (7%)
    all_gather x3, waiting for transfers between devices, local_product(): panels = lax.all_gather(panel, 'col', axis=1, tiled=True)  90.3 us
    all_gather x1, waiting for transfers between devices, local_product(): gathered_rhs = lax.all_gather(rhs_loc, 'row', axis=0)  20.7 us
    dot_general x3, matrix products, local_product(): jnp.dot(panels, rhs_steps[step], preferred_element_type=jnp.float32)  10.8 us
    slice x3, local copies, waits for them, and re-layouts, local_product(): panel = lower_loc[first_row:, step * BLOCK_SIZE:(step + 1) * BLOCK_SIZE]  5.63 us
  transfers between devices with their start and end apart: 4, of which 4 were waited for; matrix products, arithmetic and copies ran while one was open for 13% of the time, Pallas kernels for 0%

commit v1 on v0

v1 whole, which is shorter than its diff:
```python
import functools

import jax
import jax.numpy as jnp
from jax import lax
from jax.experimental import pallas as pl
from jax.experimental.pallas import tpu as pltpu
from jax.sharding import PartitionSpec as P

BLOCK = 256
CORES = 2
F32, BF16 = jnp.float32, jnp.bfloat16


def kernel(ny, nx, nt, l_hbm, b_hbm, x_out, l_v, b_v, b_all, part, far_in, end_in,
           l_sem, lsend_sem, lrecv_sem, bload_sem, xsend_sem, ysend_sem, brecv_sem, psend_sem, far_sem, end_sem):
    cols = b_hbm.shape[0]
    y = lax.axis_index("row")
    c = lax.axis_index("col")
    x, j = c // CORES, c % CORES

    def at(yy, xx, jj=j):
        return {"row": yy, "col": CORES * xx + jj}

    def remote(src, dst, send, recv, dev):
        return pltpu.make_async_remote_copy(src_ref=src, dst_ref=dst, send_sem=send, recv_sem=recv, device_id=dev,
                                            device_id_type=pl.DeviceIdType.MESH)

    xr, xl = (x + 1) % nx, (x + nx - 1) % nx
    steps = [(t, p) for t in range(nt) for p in range(2)]

    load_b = pltpu.make_async_copy(b_hbm, b_v, bload_sem)
    load_b.start()

    def l_slice(t, core):
        return (pl.ds(2 * t * BLOCK, (2 * nt - 2 * t) * BLOCK), pl.ds(pl.multiple_of((2 * t + core) * BLOCK, BLOCK), BLOCK))

    def l_src(t):
        return l_hbm.at[pl.ds(2 * t * BLOCK, (2 * nt - 2 * t) * BLOCK), pl.ds(t * BLOCK, BLOCK)]

    load_l = [pltpu.make_async_copy(l_src(t), l_v.at[l_slice(t, j)], l_sem.at[t]) for t in range(nt)]
    for copy in load_l:
        copy.start()

    barrier = pltpu.get_barrier_semaphore()
    peers = [at(y, x, 1 - j)] + [at(y, (x + d) % nx) for d in range(1, nx)] + [at((y + d) % ny, x) for d in range(1, ny)]
    for dev in peers:
        pl.semaphore_signal(barrier, inc=1, device_id=dev, device_id_type=pl.DeviceIdType.MESH)

    load_b.wait()
    pl.semaphore_wait(barrier, len(peers))

    def b_block(m):
        return b_v.at[:, pl.ds(m * BLOCK, BLOCK)]

    s_own = y % 2
    chunk_p, chunk_q = x % 2, x // 2
    for m in range(2 * nt):
        t = m // 2
        xt = y // 2 + 2 * (m % 2)
        dst = b_all.at[t, chunk_p, chunk_q, s_own]

        @pl.when(xt != x)
        def _():
            remote(b_block(m), dst, xsend_sem.at[m], brecv_sem.at[t, chunk_p, chunk_q, s_own], at(y, xt)).start()

        @pl.when(xt == x)
        def _():
            pltpu.make_async_copy(b_block(m), dst, brecv_sem.at[t, chunk_p, chunk_q, s_own]).start()

    l_copies = [remote(l_src(t), l_v.at[l_slice(t, j)], lsend_sem.at[t], lrecv_sem.at[t], at(y, x, 1 - j)) for t in range(nt)]
    for copy in l_copies:
        copy.start()

    is_holder = (y // 2) == (x % 2)
    hx = 2 * (x % 2)
    out_dir = 2 * s_own - 1
    y_partner = hx + 1 - s_own
    y_outer = (y + ny + out_dir) % ny
    y_next = (y + ny - out_dir) % ny
    s_first = is_holder.astype(jnp.int32) * s_own + (1 - is_holder.astype(jnp.int32)) * (1 - s_own)

    def recv_b(t, p, q, s):
        r = b_all.at[t, p, q, s]
        return pltpu.make_async_copy(r, r, brecv_sem.at[t, p, q, s])

    def y_copy(t, p, q, s, which, yy):
        r = b_all.at[t, p, q, s]
        return remote(r, r, ysend_sem.at[t, p, q, which], brecv_sem.at[t, p, q, s], at(yy, x))

    def forward_b(t, p):
        for q in range(2):
            recv_b(t, p, q, s_first).wait()

            @pl.when(is_holder)
            def _():
                y_copy(t, p, q, s_own, 0, y_outer).start()
                y_copy(t, p, q, s_own, 1, y_partner).start()

            @pl.when(jnp.logical_not(is_holder))
            def _():
                y_copy(t, p, q, 1 - s_own, 0, y_outer_nh).start()

    y_outer_nh = (y + ny + 1 - 2 * s_own) % ny

    def compute(t, p):
        for q in range(2):
            recv_b(t, p, q, 1 - s_first).wait()
        if p == 0:
            load_l[t].wait()
            l_copies[t].wait_recv()
        for h in range(2):
            m = 2 * t + h
            acc = jnp.zeros((2 * cols, BLOCK), F32)
            for u in range(t + 1):
                for s in range(2):
                    lhs = b_all[u, p, :, s].reshape(2 * cols, BLOCK)
                    rhs = l_v[m * BLOCK:(m + 1) * BLOCK, (2 * u + s) * BLOCK:(2 * u + s + 1) * BLOCK]
                    acc += lax.dot_general(lhs, rhs, (((1,), (1,)), ((), ())), preferred_element_type=F32)
            part[t, p, :, h] = acc.reshape(2, cols, BLOCK)

    q_own = x // 2
    q_far = 1 - q_own
    q_r, q_l = xr // 2, xl // 2

    def far_copy(t, p, h):
        return remote(part.at[t, p, q_far, h], far_in.at[t, h], psend_sem.at[t, p, h], far_sem.at[t, h], at(y, xl if h else xr))

    def end_copy(t, p, side, h):
        q, dev = (q_l, xl) if side else (q_r, xr)
        return remote(part.at[t, p, q, h], end_in.at[t, side, h], psend_sem.at[t, p, 2 * side + h], end_sem.at[t, side, h], at(y, dev))

    def first_sends(t, p):
        @pl.when(x % 2 == p)
        def _():
            far_copy(t, p, 0).start()
            far_copy(t, p, 1).start()

        @pl.when(x % 2 != p)
        def _():
            end_copy(t, p, 0, 1).start()
            end_copy(t, p, 1, 0).start()

    def merge(t, p):
        @pl.when(x % 2 != p)
        def _():
            for h, q in ((0, q_r), (1, q_l)):
                pltpu.make_async_copy(far_in.at[t, h], far_in.at[t, h], far_sem.at[t, h]).wait()
                part[t, p, q, h] += far_in[t, h]
                end_copy(t, p, h, h).start()

    def finish(t, p):
        @pl.when(x % 2 == p)
        def _():
            for h in range(2):
                for side in range(2):
                    r = end_in.at[t, side, h]
                    pltpu.make_async_copy(r, r, end_sem.at[t, side, h]).wait()
                total = part[t, p, q_own, h] + (end_in[t, 0, h] + end_in[t, 1, h])
                m = 2 * t + h
                x_out[:, m * BLOCK:(m + 1) * BLOCK] = total.astype(BF16)

    for n, (t, p) in enumerate(steps):
        forward_b(t, p)
        compute(t, p)
        first_sends(t, p)
        if n >= 1:
            merge(*steps[n - 1])
        if n >= 3:
            finish(*steps[n - 3])
    merge(*steps[-1])
    for n in range(len(steps) - 3, len(steps)):
        finish(*steps[n])

    for m in range(2 * nt):
        xt = y // 2 + 2 * (m % 2)

        @pl.when(xt != x)
        def _():
            remote(b_block(m), b_block(m), xsend_sem.at[m], xsend_sem.at[m], at(y, xt)).wait_send()
    for copy in l_copies:
        copy.wait_send()
    for t, p in steps:
        for q in range(2):
            @pl.when(is_holder)
            def _():
                y_copy(t, p, q, s_own, 0, y_outer).wait_send()
                y_copy(t, p, q, s_own, 1, y_partner).wait_send()

            @pl.when(jnp.logical_not(is_holder))
            def _():
                y_copy(t, p, q, 1 - s_own, 0, y_outer_nh).wait_send()

        @pl.when(x % 2 == p)
        def _():
            far_copy(t, p, 0).wait_send()
            far_copy(t, p, 1).wait_send()

        @pl.when(x % 2 != p)
        def _():
            for side in range(2):
                for h in range(2):
                    end_copy(t, p, side, h).wait_send()


def solution(mesh):
    ny = mesh.shape["row"]
    nx = mesh.shape["col"] // CORES

    def local_product(lower_loc, rhs_loc):
        rows, width = lower_loc.shape
        cols = rhs_loc.shape[1]
        nt = width // BLOCK
        dma = pltpu.SemaphoreType.DMA
        return pl.pallas_call(
            functools.partial(kernel, ny, nx, nt),
            out_shape=jax.ShapeDtypeStruct((cols, rows), BF16),
            in_specs=[pl.BlockSpec(memory_space=pl.ANY)] * 2,
            out_specs=pl.BlockSpec(memory_space=pltpu.VMEM),
            scratch_shapes=[
                pltpu.VMEM((rows, CORES * width), BF16),
                pltpu.VMEM((cols, rows), BF16),
                pltpu.VMEM((nt, 2, 2, 2, cols, BLOCK), BF16),
                pltpu.VMEM((nt, 2, 2, 2, cols, BLOCK), F32),
                pltpu.VMEM((nt, 2, cols, BLOCK), F32),
                pltpu.VMEM((nt, 2, 2, cols, BLOCK), F32),
                dma((nt,)), dma((nt,)), dma((nt,)), dma, dma((2 * nt,)), dma((nt, 2, 2, 2)), dma((nt, 2, 2, 2)),
                dma((nt, 2, 4)), dma((nt, 2)), dma((nt, 2, 2)),
            ],
            compiler_params=pltpu.CompilerParams(collective_id=0, has_side_effects=True),
        )(lower_loc, rhs_loc.T).T

    return jax.shard_map(local_product, mesh=mesh, in_specs=(P("row", "col"), P("row", ("batch", "col"))),
                         out_specs=P("row", ("batch", "col")), check_vma=False)
```

time: 150 us -> 55.1 us (0.37); the launches traced: 148 us -> 55 us
  waiting for transfers between devices: 112 us -> 0 us
  Pallas kernels: 0 us -> 53.3 us
  between operations: 13.2 us -> 0.01 us
  matrix products: 10.8 us -> 0 us
  local copies, waits for them, and re-layouts: 10.7 us -> 1.69 us
    all_gather x4 -> x0, waiting for transfers between devices: 111 us -> none  [the longest x3 90.3 us: local_product(): panels = lax.all_gather(panel, 'col', axis=1, tiled=True)]
    pallas_call x0 -> x1, Pallas kernels: none -> 53.3 us  [local_product(): pl.pallas_call(functools.partial(kernel, ny, nx, nt), out_shape=jax.Shape...]
    dot_general x3 -> x0, matrix products: 10.8 us -> none  [local_product(): jnp.dot(panels, rhs_steps[step], preferred_element_type=jnp.float32)]
    slice x7 -> x0, local copies, waits for them, and re-layouts: 6.93 us -> none  [the longest x3 5.63 us: local_product(): panel = lower_loc[first_row:, step * BLOCK_SIZE:(step + 1) * BLOCK_SIZE]]
    reshape x1 -> x0, local copies, waits for them, and re-layouts: 2.87 us -> none  [local_product(): gathered_rhs.reshape(grid_rows, row_blocks, BLOCK_SIZE, rhs_cols)]
    unnamed x0 -> x1, local copies, waits for them, and re-layouts: none -> 1.69 us
  transfers between devices with their start and end apart: 4 -> 0, of which waited for: 4 -> 0; matrix products, arithmetic and copies ran while one was open for 13% -> 0% of each run, Pallas kernels for 0% -> 0%
where the time goes in v1:
time: 55.1 us; the launch traced here: 55 us
  Pallas kernels  53.3 us (97%)
  local copies, waits for them, and re-layouts  1.69 us (3%)
    pallas_call x1, Pallas kernels, local_product(): pl.pallas_call(functools.partial(kernel, ny, nx, nt), out_shape=jax.Shape...  53.3 us
    unnamed x1, local copies, waits for them, and re-layouts  1.69 us

profile of v1, /device:TPU:98, one launch (start us, length us, event | category | flops | bytes accessed | tf_op | source)
XLA Modules:
  0.0 55.0 jit_solution(15614378868075284812)
XLA Ops:
  0.0 53.3 %shard_map.28 = bf16[96,1536]{1,0:T(8,128)(2,1)} custom-call(bf16[1536,768]{1,0:T(8,128)(2,1)} %l_hbm.1, bf16[96,1536]{1,0:T(8,128)(2,1)} %bitcast.3), custom_call_target="tpu_custom_call" | custom-call | tf_op jit(solution)/shard_map/pallas_call | solution.py:215
  53.3 1.7 %copy.4 = bf16[1536,96]{0,1:T(8,128)(2,1)} copy(bf16[1536,96]{0,1:T(8,128)(2,1)} %bitcast.2) | data formatting | bytes 589824

commit v2 on v1

--- a/solution.py
+++ b/solution.py
@@ -88,17 +88,19 @@
         r = b_all.at[t, p, q, s]
         return remote(r, r, ysend_sem.at[t, p, q, which], brecv_sem.at[t, p, q, s], at(yy, x))
 
-    def forward_b(t, p):
-        for q in range(2):
-            recv_b(t, p, q, s_first).wait()
-
-            @pl.when(is_holder)
-            def _():
+    def forward_held(t, p):
+        @pl.when(is_holder)
+        def _():
+            for q in range(2):
+                recv_b(t, p, q, s_own).wait()
                 y_copy(t, p, q, s_own, 0, y_outer).start()
                 y_copy(t, p, q, s_own, 1, y_partner).start()
 
-            @pl.when(jnp.logical_not(is_holder))
-            def _():
+    def forward_passed(t, p):
+        @pl.when(jnp.logical_not(is_holder))
+        def _():
+            for q in range(2):
+                recv_b(t, p, q, 1 - s_own).wait()
                 y_copy(t, p, q, 1 - s_own, 0, y_outer_nh).start()
 
     y_outer_nh = (y + ny + 1 - 2 * s_own) % ny
@@ -160,8 +162,12 @@
                 m = 2 * t + h
                 x_out[:, m * BLOCK:(m + 1) * BLOCK] = total.astype(BF16)
 
+    for t, p in steps:
+        forward_held(t, p)
+    forward_passed(*steps[0])
     for n, (t, p) in enumerate(steps):
-        forward_b(t, p)
+        if n + 1 < len(steps):
+            forward_passed(*steps[n + 1])
         compute(t, p)
         first_sends(t, p)
         if n >= 1:
@@ -214,7 +220,7 @@
         dma = pltpu.SemaphoreType.DMA
         return pl.pallas_call(
             functools.partial(kernel, ny, nx, nt),
-            out_shape=jax.ShapeDtypeStruct((cols, rows), BF16),
+            out_shape=pltpu.VMEM((cols, rows), BF16),
             in_specs=[pl.BlockSpec(memory_space=pl.ANY)] * 2,
             out_specs=pl.BlockSpec(memory_space=pltpu.VMEM),
             scratch_shapes=[

time: 55.1 us -> 44.7 us (0.81)
  Pallas kernels: 53.3 us -> 43.9 us
  local copies, waits for them, and re-layouts: 1.69 us -> 0.72 us
    pallas_call x1, Pallas kernels: 53.3 us -> 43.9 us  [local_product(): pl.pallas_call(functools.partial(kernel, ny, nx, nt), out_shape=pltpu.VME...]
    unnamed x1, local copies, waits for them, and re-layouts: 1.69 us -> 0.72 us
where the time goes in v2:
time: 44.7 us; the launch traced here: 44.6 us
  Pallas kernels  43.9 us (98%)
  local copies, waits for them, and re-layouts  0.72 us (2%)
    pallas_call x1, Pallas kernels, local_product(): pl.pallas_call(functools.partial(kernel, ny, nx, nt), out_shape=pltpu.VME...  43.9 us

profile of v2, /device:TPU:98, one launch (start us, length us, event | category | flops | bytes accessed | tf_op | source)
XLA Modules:
  0.0 44.6 jit_solution(16812638473810591201)
XLA Ops:
  0.0 43.9 %shard_map.28 = bf16[96,1536]{1,0:T(8,128)(2,1)S(1)} custom-call(bf16[1536,768]{1,0:T(8,128)(2,1)} %l_hbm.1, bf16[96,1536]{1,0:T(8,128)(2,1)} %bitcast.3), custom_call_target="tpu_custom_call" | custom-call | tf_op jit(solution)/shard_map/pallas_call | solution.py:221
  43.9 0.7 %copy.4 = bf16[1536,96]{0,1:T(8,128)(2,1)} copy(bf16[1536,96]{0,1:T(8,128)(2,1)S(1)} %bitcast.2) | data formatting | bytes 589824

commit v3 on v0

v3 whole, which is shorter than its diff:
```python
import functools

import jax
import jax.numpy as jnp
from jax import lax
from jax.experimental import pallas as pl
from jax.experimental.pallas import tpu as pltpu
from jax.sharding import PartitionSpec as P

BLOCK = 256
CORES = 2
F32, BF16 = jnp.float32, jnp.bfloat16


def kernel(ny, nx, nt, l_hbm, b_hbm, x_out, l_v, b_v, b_col, b_all, part, far_in, end_in, l_sem, lsend, lrecv, bload, gsend, grecv,
           xsend, ysend, brecv, psend, far_sem, end_sem):
    cols = b_hbm.shape[0]
    y = lax.axis_index("row")
    c = lax.axis_index("col")
    x, j = c // CORES, c % CORES

    def at(yy, xx, jj=j):
        return {"row": yy, "col": CORES * xx + jj}

    def remote(src, dst, send, recv, dev):
        return pltpu.make_async_remote_copy(src_ref=src, dst_ref=dst, send_sem=send, recv_sem=recv, device_id=dev,
                                            device_id_type=pl.DeviceIdType.MESH)

    def landed(ref, sem):
        pltpu.make_async_copy(ref, ref, sem).wait()

    xr, xl = (x + 1) % nx, (x + nx - 1) % nx
    yu, yd = (y + 1) % ny, (y + ny - 1) % ny
    p_end, p_mid = x % 2, 1 - x % 2

    load_b = pltpu.make_async_copy(b_hbm, b_v, bload)
    load_b.start()

    def l_slice(t, core):
        return (pl.ds(2 * t * BLOCK, (2 * nt - 2 * t) * BLOCK), pl.ds(pl.multiple_of((2 * t + core) * BLOCK, BLOCK), BLOCK))

    def l_src(t):
        return l_hbm.at[pl.ds(2 * t * BLOCK, (2 * nt - 2 * t) * BLOCK), pl.ds(t * BLOCK, BLOCK)]

    load_l = [pltpu.make_async_copy(l_src(t), l_v.at[l_slice(t, j)], l_sem.at[t]) for t in range(nt)]
    for copy in load_l:
        copy.start()

    barrier = pltpu.get_barrier_semaphore()
    peers = [at(y, x, 1 - j)] + [at(y, (x + d) % nx) for d in range(1, nx)] + [at(yu, x), at(yd, x)]
    for dev in peers:
        pl.semaphore_signal(barrier, inc=1, device_id=dev, device_id_type=pl.DeviceIdType.MESH)
    load_b.wait()
    pl.semaphore_wait(barrier, len(peers))

    def b_block(m):
        return b_v.at[:, pl.ds(m * BLOCK, BLOCK)]

    s_own = y % 2
    chunk_p, chunk_q = x % 2, x // 2

    def gather_copy(m, yy, i):
        k = ny * m + y
        return remote(b_block(m), b_col.at[k], gsend.at[i], grecv.at[k], at(yy, x))

    def pass_copy(m, y_from, y_to, i):
        r = b_col.at[ny * m + y_from]
        return remote(r, r, gsend.at[i], grecv.at[ny * m + y_from], at(y_to, x))

    gathers = [gather_copy(0, yu, 0), gather_copy(1, yd, 1), gather_copy(1, yu, 2), gather_copy(0, yd, 3)]
    passes = [pass_copy(0, yd, yu, 4), pass_copy(1, yu, yd, 5)]

    def place_copy(m, d):
        yy = (y + d) % ny
        src = b_col.at[ny * m + yy] if d else b_block(m)
        dst, sem = b_all.at[0, chunk_p, chunk_q, yy % 2], brecv.at[0, chunk_p, chunk_q, yy % 2]
        xt = yy // 2 + 2 * m
        return xt, (lambda: remote(src, dst, gsend.at[6 + ny * m + d], sem, at(y, xt))), (lambda: pltpu.make_async_copy(src, dst, sem))

    def came(m, d):
        k = ny * m + (y + d) % ny
        landed(b_col.at[k], grecv.at[k])

    def place(m, d):
        xt, away, here = place_copy(m, d)

        @pl.when(xt != x)
        def _():
            away().start()

        @pl.when(xt == x)
        def _():
            here().start()

    def x_copy(m):
        xt = y // 2 + 2 * (m % 2)
        dst, sem = b_all.at[m // 2, chunk_p, chunk_q, s_own], brecv.at[m // 2, chunk_p, chunk_q, s_own]
        return xt, (lambda: remote(b_block(m), dst, xsend.at[m], sem, at(y, xt))), (lambda: pltpu.make_async_copy(b_block(m), dst, sem))

    def x_first(t):
        for m in (2 * t, 2 * t + 1):
            xt, away, here = x_copy(m)

            @pl.when(xt != x)
            def _():
                away().start()

            @pl.when(xt == x)
            def _():
                here().start()

    is_holder = (y // 2) == (x % 2)
    hx = 2 * (x % 2)
    y_partner = hx + 1 - s_own
    y_outer = (y + ny + 2 * s_own - 1) % ny
    y_next = (y + ny + 1 - 2 * s_own) % ny
    held = is_holder.astype(jnp.int32)
    s_first = held * s_own + (1 - held) * (1 - s_own)

    def y_copy(t, p, q, s, which, yy):
        r = b_all.at[t, p, q, s]
        return remote(r, r, ysend.at[t, p, q, which], brecv.at[t, p, q, s], at(yy, x))

    def b_came(t, p, q, s):
        landed(b_all.at[t, p, q, s], brecv.at[t, p, q, s])

    def forward_held(t):
        @pl.when(is_holder)
        def _():
            for p in (p_end, p_mid):
                for q in range(2):
                    b_came(t, p, q, s_own)
                    y_copy(t, p, q, s_own, 0, y_outer).start()
                    y_copy(t, p, q, s_own, 1, y_partner).start()

    def forward_passed(t, p):
        @pl.when(jnp.logical_not(is_holder))
        def _():
            for q in range(2):
                b_came(t, p, q, 1 - s_own)
                y_copy(t, p, q, 1 - s_own, 0, y_next).start()

    def compute(t, role):
        p = (p_end, p_mid)[role]
        for q in range(2):
            for s in range(2) if t == 0 else (1 - s_first,):
                b_came(t, p, q, s)
        if role == 0:
            load_l[t].wait()
            l_copies[t].wait_recv()
        for h in range(2):
            m = 2 * t + h
            acc = jnp.zeros((2 * cols, BLOCK), F32)
            for u in range(t + 1):
                for s in range(2):
                    lhs = b_all[u, p, :, s].reshape(2 * cols, BLOCK)
                    rhs = l_v[m * BLOCK:(m + 1) * BLOCK, (2 * u + s) * BLOCK:(2 * u + s + 1) * BLOCK]
                    acc += lax.dot_general(lhs, rhs, (((1,), (1,)), ((), ())), preferred_element_type=F32)
            part[t, role, :, h] = acc.reshape(2, cols, BLOCK)

    q_own = x // 2

    def far_copy(t, h):
        return remote(part.at[t, 0, 1 - q_own, h], far_in.at[t, h], psend.at[t, h], far_sem.at[t, h], at(y, xl if h else xr))

    def end_copy(t, side, h):
        xx = xl if side else xr
        return remote(part.at[t, 1, xx // 2, h], end_in.at[t, side, h], psend.at[t, 2 + 2 * side + h], end_sem.at[t, side, h], at(y, xx))

    def ends(t):
        compute(t, 0)
        far_copy(t, 0).start()
        far_copy(t, 1).start()

    def middles(t):
        compute(t, 1)
        end_copy(t, 0, 1).start()
        end_copy(t, 1, 0).start()

    def merge(t):
        for h, xx in ((0, xr), (1, xl)):
            landed(far_in.at[t, h], far_sem.at[t, h])
            part[t, 1, xx // 2, h] += far_in[t, h]
            end_copy(t, h, h).start()

    def finish(t, h):
        for side in range(2):
            landed(end_in.at[t, side, h], end_sem.at[t, side, h])
        m = 2 * t + h
        x_out[:, m * BLOCK:(m + 1) * BLOCK] = (part[t, 0, q_own, h] + (end_in[t, 0, h] + end_in[t, 1, h])).astype(BF16)

    l_copies = [remote(l_src(t), l_v.at[l_slice(t, j)], lsend.at[t], lrecv.at[t], at(y, x, 1 - j)) for t in range(nt)]
    for copy in gathers:
        copy.start()
    place(0, 0)
    place(1, 0)
    x_first(1)
    for copy in l_copies:
        copy.start()
    came(0, ny - 1)
    passes[0].start()
    place(0, ny - 1)
    came(1, 1)
    passes[1].start()
    place(1, 1)
    came(1, ny - 1)
    place(1, ny - 1)
    came(0, 1)
    place(0, 1)
    for m in range(2):
        came(m, 2)
        place(m, 2)
    for t in range(2, nt):
        x_first(t)
    forward_held(1)
    ends(0)
    middles(0)
    forward_passed(1, p_end)
    forward_passed(1, p_mid)
    merge(0)
    forward_held(2)
    ends(1)
    middles(1)
    forward_passed(2, p_end)
    forward_passed(2, p_mid)
    merge(1)
    for h in range(2):
        finish(0, h)
    ends(2)
    middles(2)
    merge(2)
    for h in range(2):
        finish(1, h)

    for copy in gathers + passes + l_copies:
        copy.wait_send()
    for m in range(2):
        for d in range(ny):
            xt, away, _ = place_copy(m, d)

            @pl.when(xt != x)
            def _():
                away().wait_send()
    for m in range(2, 2 * nt):
        xt, away, _ = x_copy(m)

        @pl.when(xt != x)
        def _():
            away().wait_send()
    for t in range(1, nt):
        for p in range(2):
            for q in range(2):
                @pl.when(is_holder)
                def _():
                    y_copy(t, p, q, s_own, 0, y_outer).wait_send()
                    y_copy(t, p, q, s_own, 1, y_partner).wait_send()

                @pl.when(jnp.logical_not(is_holder))
                def _():
                    y_copy(t, p, q, 1 - s_own, 0, y_next).wait_send()
    for t in range(nt):
        for h in range(2):
            far_copy(t, h).wait_send()
            end_copy(t, 1 - h, h).wait_send()
    for t in range(nt - 1):
        for h in range(2):
            end_copy(t, h, h).wait_send()
    for h in range(2):
        finish(nt - 1, h)
    for h in range(2):
        end_copy(nt - 1, h, h).wait_send()


def solution(mesh):
    ny = mesh.shape["row"]
    nx = mesh.shape["col"] // CORES

    def local_product(lower_loc, rhs_loc):
        rows, width = lower_loc.shape
        cols = rhs_loc.shape[1]
        nt = width // BLOCK
        dma = pltpu.SemaphoreType.DMA
        return pl.pallas_call(
            functools.partial(kernel, ny, nx, nt),
            out_shape=pltpu.VMEM((cols, rows), BF16),
            in_specs=[pl.BlockSpec(memory_space=pl.ANY)] * 2,
            out_specs=pl.BlockSpec(memory_space=pltpu.VMEM),
            scratch_shapes=[
                pltpu.VMEM((rows, CORES * width), BF16),
                pltpu.VMEM((cols, rows), BF16),
                pltpu.VMEM((2 * ny, cols, BLOCK), BF16),
                pltpu.VMEM((nt, 2, 2, 2, cols, BLOCK), BF16),
                pltpu.VMEM((nt, 2, 2, 2, cols, BLOCK), F32),
                pltpu.VMEM((nt, 2, cols, BLOCK), F32),
                pltpu.VMEM((nt, 2, 2, cols, BLOCK), F32),
                dma((nt,)), dma((nt,)), dma((nt,)), dma, dma((6 + 2 * ny,)), dma((2 * ny,)), dma((2 * nt,)),
                dma((nt, 2, 2, 2)), dma((nt, 2, 2, 2)), dma((nt, 6)), dma((nt, 2)), dma((nt, 2, 2)),
            ],
            compiler_params=pltpu.CompilerParams(collective_id=0, has_side_effects=True),
        )(lower_loc, rhs_loc.T).T

    return jax.shard_map(local_product, mesh=mesh, in_specs=(P("row", "col"), P("row", ("batch", "col"))),
                         out_specs=P("row", ("batch", "col")), check_vma=False)
```

time: 150 us -> 39.5 us (0.26); the launches traced: 148 us -> 39.4 us
  waiting for transfers between devices: 112 us -> 0 us
  Pallas kernels: 0 us -> 38.7 us
  between operations: 13.2 us -> 0.01 us
  matrix products: 10.8 us -> 0 us
  local copies, waits for them, and re-layouts: 10.7 us -> 0.72 us
    all_gather x4 -> x0, waiting for transfers between devices: 111 us -> none  [the longest x3 90.3 us: local_product(): panels = lax.all_gather(panel, 'col', axis=1, tiled=True)]
    pallas_call x0 -> x1, Pallas kernels: none -> 38.7 us  [local_product(): pl.pallas_call(functools.partial(kernel, ny, nx, nt), out_shape=pltpu.VME...]
    dot_general x3 -> x0, matrix products: 10.8 us -> none  [local_product(): jnp.dot(panels, rhs_steps[step], preferred_element_type=jnp.float32)]
    slice x7 -> x0, local copies, waits for them, and re-layouts: 6.93 us -> none  [the longest x3 5.63 us: local_product(): panel = lower_loc[first_row:, step * BLOCK_SIZE:(step + 1) * BLOCK_SIZE]]
    reshape x1 -> x0, local copies, waits for them, and re-layouts: 2.87 us -> none  [local_product(): gathered_rhs.reshape(grid_rows, row_blocks, BLOCK_SIZE, rhs_cols)]
  transfers between devices with their start and end apart: 4 -> 0, of which waited for: 4 -> 0; matrix products, arithmetic and copies ran while one was open for 13% -> 0% of each run, Pallas kernels for 0% -> 0%
where the time goes in v3:
time: 39.5 us; the launch traced here: 39.4 us
  Pallas kernels  38.7 us (98%)
  local copies, waits for them, and re-layouts  0.72 us (2%)
    pallas_call x1, Pallas kernels, local_product(): pl.pallas_call(functools.partial(kernel, ny, nx, nt), out_shape=pltpu.VME...  38.7 us

profile of v3, /device:TPU:98, one launch (start us, length us, event | category | flops | bytes accessed | tf_op | source)
XLA Modules:
  0.0 39.4 jit_solution(2112049814034782598)
XLA Ops:
  0.0 38.7 %shard_map.28 = bf16[96,1536]{1,0:T(8,128)(2,1)S(1)} custom-call(bf16[1536,768]{1,0:T(8,128)(2,1)} %l_hbm.1, bf16[96,1536]{1,0:T(8,128)(2,1)} %bitcast.3), custom_call_target="tpu_custom_call" | custom-call | tf_op jit(solution)/shard_map/pallas_call | solution.py:283
  38.7 0.7 %copy.4 = bf16[1536,96]{0,1:T(8,128)(2,1)} copy(bf16[1536,96]{0,1:T(8,128)(2,1)S(1)} %bitcast.2) | data formatting | bytes 589824

commit v4 on v3

--- a/solution.py
+++ b/solution.py
@@ -7,6 +7,10 @@
 from jax.experimental.pallas import tpu as pltpu
 from jax.sharding import PartitionSpec as P
 
+ORDER = (
+    "g", "p0", "x1", "L", "a01", "a03", "a11", "a13", "x2", "a02", "a12", "h1", "E0", "M0", "h2", "fe1",
+    "fm1", "G0", "E1", "M1", "fe2", "fm2", "E2", "M2", "G1", "F0", "G2", "F1",
+)
 BLOCK = 256
 CORES = 2
 F32, BF16 = jnp.float32, jnp.bfloat16
@@ -67,8 +71,8 @@
         r = b_col.at[ny * m + y_from]
         return remote(r, r, gsend.at[i], grecv.at[ny * m + y_from], at(y_to, x))
 
-    gathers = [gather_copy(0, yu, 0), gather_copy(1, yd, 1), gather_copy(1, yu, 2), gather_copy(0, yd, 3)]
-    passes = [pass_copy(0, yd, yu, 4), pass_copy(1, yu, yd, 5)]
+    gathers = [gather_copy(0, yu, 0), gather_copy(0, yd, 1), gather_copy(1, yu, 2), gather_copy(1, yd, 3)]
+    passes = [pass_copy(1, yd, yu, 4), pass_copy(0, yu, yd, 5)]
 
     def place_copy(m, d):
         yy = (y + d) % ny
@@ -142,14 +146,36 @@
 
     def compute(t, role):
         p = (p_end, p_mid)[role]
-        for q in range(2):
-            for s in range(2) if t == 0 else (1 - s_first,):
-                b_came(t, p, q, s)
+        if t == 0:
+            for s in range(2):
+                @pl.when(CORES * x + s <= y + ny)
+                def _():
+                    for q in range(2):
+                        b_came(t, p, q, s)
+        else:
+            for q in range(2):
+                b_came(t, p, q, 1 - s_first)
+        if t == 1:
+            for s in range(2):
+                @pl.when(CORES * x + s > y + ny)
+                def _():
+                    for q in range(2):
+                        b_came(0, p, q, s)
         if role == 0:
             load_l[t].wait()
             l_copies[t].wait_recv()
         for h in range(2):
             m = 2 * t + h
+            if t == 0:
+                part[t, role, :, h] = jnp.zeros((2, cols, BLOCK), F32)
+                for s in range(2):
+                    @pl.when(CORES * x + s <= y + ny * h)
+                    def _():
+                        lhs = b_all[0, p, :, s].reshape(2 * cols, BLOCK)
+                        rhs = l_v[m * BLOCK:(m + 1) * BLOCK, s * BLOCK:(s + 1) * BLOCK]
+                        acc = lax.dot_general(lhs, rhs, (((1,), (1,)), ((), ())), preferred_element_type=F32)
+                        part[t, role, :, h] += acc.reshape(2, cols, BLOCK)
+                continue
             acc = jnp.zeros((2 * cols, BLOCK), F32)
             for u in range(t + 1):
                 for s in range(2):
@@ -190,47 +216,39 @@
         x_out[:, m * BLOCK:(m + 1) * BLOCK] = (part[t, 0, q_own, h] + (end_in[t, 0, h] + end_in[t, 1, h])).astype(BF16)
 
     l_copies = [remote(l_src(t), l_v.at[l_slice(t, j)], lsend.at[t], lrecv.at[t], at(y, x, 1 - j)) for t in range(nt)]
-    for copy in gathers:
-        copy.start()
-    place(0, 0)
-    place(1, 0)
-    x_first(1)
-    for copy in l_copies:
-        copy.start()
-    came(0, ny - 1)
-    passes[0].start()
-    place(0, ny - 1)
-    came(1, 1)
-    passes[1].start()
-    place(1, 1)
-    came(1, ny - 1)
-    place(1, ny - 1)
-    came(0, 1)
-    place(0, 1)
-    for m in range(2):
-        came(m, 2)
-        place(m, 2)
-    for t in range(2, nt):
-        x_first(t)
-    forward_held(1)
-    ends(0)
-    middles(0)
-    forward_passed(1, p_end)
-    forward_passed(1, p_mid)
-    merge(0)
-    forward_held(2)
-    ends(1)
-    middles(1)
-    forward_passed(2, p_end)
-    forward_passed(2, p_mid)
-    merge(1)
-    for h in range(2):
-        finish(0, h)
-    ends(2)
-    middles(2)
-    merge(2)
-    for h in range(2):
-        finish(1, h)
+    def start_all(copies):
+        for copy in copies:
+            copy.start()
+
+    def arrive(m, d, fwd=None):
+        came(m, d)
+        if fwd is not None:
+            passes[fwd].start()
+        place(m, d)
+
+    items = {
+        "g": lambda: start_all(gathers),
+        "p0": lambda: (place(0, 0), place(1, 0)),
+        "L": lambda: start_all(l_copies),
+        "a01": lambda: arrive(0, 1, 1),
+        "a13": lambda: arrive(1, ny - 1, 0),
+        "a11": lambda: arrive(1, 1),
+        "a03": lambda: arrive(0, ny - 1),
+        "a02": lambda: arrive(0, 2),
+        "a12": lambda: arrive(1, 2),
+    }
+    for t in range(1, nt):
+        items["x%d" % t] = functools.partial(x_first, t)
+        items["h%d" % t] = functools.partial(forward_held, t)
+        items["fe%d" % t] = functools.partial(forward_passed, t, p_end)
+        items["fm%d" % t] = functools.partial(forward_passed, t, p_mid)
+    for t in range(nt):
+        items["E%d" % t] = functools.partial(ends, t)
+        items["M%d" % t] = functools.partial(middles, t)
+        items["G%d" % t] = functools.partial(merge, t)
+        items["F%d" % t] = lambda t=t: [finish(t, h) for h in range(2)]
+    for name in ORDER:
+        items[name]()
 
     for copy in gathers + passes + l_copies:
         copy.wait_send()

time: 39.5 us -> 37.8 us (0.957)
  Pallas kernels: 38.7 us -> 36.9 us
    pallas_call x1, Pallas kernels: 38.7 us -> 36.9 us  [local_product(): pl.pallas_call(functools.partial(kernel, ny, nx, nt), out_shape=pltpu.VME...]
where the time goes in v4:
time: 37.8 us; the launch traced here: 37.7 us
  Pallas kernels  36.9 us (98%)
  local copies, waits for them, and re-layouts  0.72 us (2%)
    pallas_call x1, Pallas kernels, local_product(): pl.pallas_call(functools.partial(kernel, ny, nx, nt), out_shape=pltpu.VME...  36.9 us

profile of v4, /device:TPU:98, one launch (start us, length us, event | category | flops | bytes accessed | tf_op | source)
XLA Modules:
  0.0 37.7 jit_solution(10495398230647262746)
XLA Ops:
  0.0 36.9 %shard_map.28 = bf16[96,1536]{1,0:T(8,128)(2,1)S(1)} custom-call(bf16[1536,768]{1,0:T(8,128)(2,1)} %l_hbm.1, bf16[96,1536]{1,0:T(8,128)(2,1)} %bitcast.3), custom_call_target="tpu_custom_call" | custom-call | tf_op jit(solution)/shard_map/pallas_call | solution.py:301
  36.9 0.7 %copy.4 = bf16[1536,96]{0,1:T(8,128)(2,1)} copy(bf16[1536,96]{0,1:T(8,128)(2,1)S(1)} %bitcast.2) | data formatting | bytes 589824

commit v5 on v4

--- a/solution.py
+++ b/solution.py
@@ -9,15 +9,15 @@
 
 ORDER = (
     "g", "p0", "x1", "L", "a01", "a03", "a11", "a13", "x2", "a02", "a12", "h1", "E0", "M0", "h2", "fe1",
-    "fm1", "G0", "E1", "M1", "fe2", "fm2", "E2", "M2", "G1", "F0", "G2", "F1",
+    "fm1", "G0", "E1", "fe2", "M1", "fm2", "E2", "M2", "G1", "F0", "G2", "F1",
 )
 BLOCK = 256
 CORES = 2
 F32, BF16 = jnp.float32, jnp.bfloat16
 
 
-def kernel(ny, nx, nt, l_hbm, b_hbm, x_out, l_v, b_v, b_col, b_all, part, far_in, end_in, l_sem, lsend, lrecv, bload, gsend, grecv,
-           xsend, ysend, brecv, psend, far_sem, end_sem):
+def kernel(ny, nx, nt, l_hbm, b_hbm, x_out, l_v, b_v, b_col, b_all, part, far_in, end_in, l_sem, lsend, lrecv, bload, gsend, psem,
+           xsend, ysend, fsend, esend, grecv, brecv, far_sem, end_sem):
     cols = b_hbm.shape[0]
     y = lax.axis_index("row")
     c = lax.axis_index("col")
@@ -46,7 +46,7 @@
     def l_src(t):
         return l_hbm.at[pl.ds(2 * t * BLOCK, (2 * nt - 2 * t) * BLOCK), pl.ds(t * BLOCK, BLOCK)]
 
-    load_l = [pltpu.make_async_copy(l_src(t), l_v.at[l_slice(t, j)], l_sem.at[t]) for t in range(nt)]
+    load_l = [pltpu.make_async_copy(l_src(t), l_v.at[l_slice(t, j)], l_sem) for t in range(nt)]
     for copy in load_l:
         copy.start()
 
@@ -65,11 +65,11 @@
 
     def gather_copy(m, yy, i):
         k = ny * m + y
-        return remote(b_block(m), b_col.at[k], gsend.at[i], grecv.at[k], at(yy, x))
+        return remote(b_block(m), b_col.at[k], gsend, grecv.at[k], at(yy, x))
 
     def pass_copy(m, y_from, y_to, i):
         r = b_col.at[ny * m + y_from]
-        return remote(r, r, gsend.at[i], grecv.at[ny * m + y_from], at(y_to, x))
+        return remote(r, r, gsend, grecv.at[ny * m + y_from], at(y_to, x))
 
     gathers = [gather_copy(0, yu, 0), gather_copy(0, yd, 1), gather_copy(1, yu, 2), gather_copy(1, yd, 3)]
     passes = [pass_copy(1, yd, yu, 4), pass_copy(0, yu, yd, 5)]
@@ -77,9 +77,9 @@
     def place_copy(m, d):
         yy = (y + d) % ny
         src = b_col.at[ny * m + yy] if d else b_block(m)
-        dst, sem = b_all.at[0, chunk_p, chunk_q, yy % 2], brecv.at[0, chunk_p, chunk_q, yy % 2]
+        dst, sem = b_all.at[0, chunk_p, yy % 2, chunk_q], brecv.at[0, chunk_p, yy % 2, chunk_q]
         xt = yy // 2 + 2 * m
-        return xt, (lambda: remote(src, dst, gsend.at[6 + ny * m + d], sem, at(y, xt))), (lambda: pltpu.make_async_copy(src, dst, sem))
+        return xt, (lambda: remote(src, dst, psem, sem, at(y, xt))), (lambda: pltpu.make_async_copy(src, dst, sem))
 
     def came(m, d):
         k = ny * m + (y + d) % ny
@@ -98,8 +98,8 @@
 
     def x_copy(m):
         xt = y // 2 + 2 * (m % 2)
-        dst, sem = b_all.at[m // 2, chunk_p, chunk_q, s_own], brecv.at[m // 2, chunk_p, chunk_q, s_own]
-        return xt, (lambda: remote(b_block(m), dst, xsend.at[m], sem, at(y, xt))), (lambda: pltpu.make_async_copy(b_block(m), dst, sem))
+        dst, sem = b_all.at[m // 2, chunk_p, s_own, chunk_q], brecv.at[m // 2, chunk_p, s_own, chunk_q]
+        return xt, (lambda: remote(b_block(m), dst, xsend, sem, at(y, xt))), (lambda: pltpu.make_async_copy(b_block(m), dst, sem))
 
     def x_first(t):
         for m in (2 * t, 2 * t + 1):
@@ -121,28 +121,28 @@
     held = is_holder.astype(jnp.int32)
     s_first = held * s_own + (1 - held) * (1 - s_own)
 
-    def y_copy(t, p, q, s, which, yy):
-        r = b_all.at[t, p, q, s]
-        return remote(r, r, ysend.at[t, p, q, which], brecv.at[t, p, q, s], at(yy, x))
-
-    def b_came(t, p, q, s):
-        landed(b_all.at[t, p, q, s], brecv.at[t, p, q, s])
+    def y_copy(t, p, s, q, yy):
+        r = b_all.at[t, p, s, q]
+        return remote(r, r, ysend, brecv.at[t, p, s, q], at(yy, x))
+
+    def b_came(t, p, s, q):
+        landed(b_all.at[t, p, s, q], brecv.at[t, p, s, q])
 
     def forward_held(t):
         @pl.when(is_holder)
         def _():
             for p in (p_end, p_mid):
                 for q in range(2):
-                    b_came(t, p, q, s_own)
-                    y_copy(t, p, q, s_own, 0, y_outer).start()
-                    y_copy(t, p, q, s_own, 1, y_partner).start()
+                    b_came(t, p, s_own, q)
+                    y_copy(t, p, s_own, q, y_outer).start()
+                    y_copy(t, p, s_own, q, y_partner).start()
 
     def forward_passed(t, p):
         @pl.when(jnp.logical_not(is_holder))
         def _():
             for q in range(2):
-                b_came(t, p, q, 1 - s_own)
-                y_copy(t, p, q, 1 - s_own, 0, y_next).start()
+                b_came(t, p, 1 - s_own, q)
+                y_copy(t, p, 1 - s_own, q, y_next).start()
 
     def compute(t, role):
         p = (p_end, p_mid)[role]
@@ -151,19 +151,20 @@
                 @pl.when(CORES * x + s <= y + ny)
                 def _():
                     for q in range(2):
-                        b_came(t, p, q, s)
+                        b_came(t, p, s, q)
         else:
             for q in range(2):
-                b_came(t, p, q, 1 - s_first)
+                b_came(t, p, 1 - s_first, q)
         if t == 1:
             for s in range(2):
                 @pl.when(CORES * x + s > y + ny)
                 def _():
                     for q in range(2):
-                        b_came(0, p, q, s)
-        if role == 0:
-            load_l[t].wait()
-            l_copies[t].wait_recv()
+                        b_came(0, p, s, q)
+        if role == 0 and t == 0:
+            l_all = l_v.at[pl.ds(0, (nt + 1) * BLOCK // 2), :]
+            landed(l_all, l_sem)
+            landed(l_all, lrecv)
         for h in range(2):
             m = 2 * t + h
             if t == 0:
@@ -171,7 +172,7 @@
                 for s in range(2):
                     @pl.when(CORES * x + s <= y + ny * h)
                     def _():
-                        lhs = b_all[0, p, :, s].reshape(2 * cols, BLOCK)
+                        lhs = b_all[0, p, s].reshape(2 * cols, BLOCK)
                         rhs = l_v[m * BLOCK:(m + 1) * BLOCK, s * BLOCK:(s + 1) * BLOCK]
                         acc = lax.dot_general(lhs, rhs, (((1,), (1,)), ((), ())), preferred_element_type=F32)
                         part[t, role, :, h] += acc.reshape(2, cols, BLOCK)
@@ -179,7 +180,7 @@
             acc = jnp.zeros((2 * cols, BLOCK), F32)
             for u in range(t + 1):
                 for s in range(2):
-                    lhs = b_all[u, p, :, s].reshape(2 * cols, BLOCK)
+                    lhs = b_all[u, p, s].reshape(2 * cols, BLOCK)
                     rhs = l_v[m * BLOCK:(m + 1) * BLOCK, (2 * u + s) * BLOCK:(2 * u + s + 1) * BLOCK]
                     acc += lax.dot_general(lhs, rhs, (((1,), (1,)), ((), ())), preferred_element_type=F32)
             part[t, role, :, h] = acc.reshape(2, cols, BLOCK)
@@ -187,11 +188,11 @@
     q_own = x // 2
 
     def far_copy(t, h):
-        return remote(part.at[t, 0, 1 - q_own, h], far_in.at[t, h], psend.at[t, h], far_sem.at[t, h], at(y, xl if h else xr))
+        return remote(part.at[t, 0, 1 - q_own, h], far_in.at[t, h], fsend, far_sem.at[t, h], at(y, xl if h else xr))
 
     def end_copy(t, side, h):
         xx = xl if side else xr
-        return remote(part.at[t, 1, xx // 2, h], end_in.at[t, side, h], psend.at[t, 2 + 2 * side + h], end_sem.at[t, side, h], at(y, xx))
+        return remote(part.at[t, 1, xx // 2, h], end_in.at[t, h, side], esend, end_sem.at[t, h], at(y, xx))
 
     def ends(t):
         compute(t, 0)
@@ -210,12 +211,11 @@
             end_copy(t, h, h).start()
 
     def finish(t, h):
-        for side in range(2):
-            landed(end_in.at[t, side, h], end_sem.at[t, side, h])
+        landed(end_in.at[t, h], end_sem.at[t, h])
         m = 2 * t + h
-        x_out[:, m * BLOCK:(m + 1) * BLOCK] = (part[t, 0, q_own, h] + (end_in[t, 0, h] + end_in[t, 1, h])).astype(BF16)
-
-    l_copies = [remote(l_src(t), l_v.at[l_slice(t, j)], lsend.at[t], lrecv.at[t], at(y, x, 1 - j)) for t in range(nt)]
+        x_out[:, m * BLOCK:(m + 1) * BLOCK] = (part[t, 0, q_own, h] + (end_in[t, h, 0] + end_in[t, h, 1])).astype(BF16)
+
+    l_copies = [remote(l_src(t), l_v.at[l_slice(t, j)], lsend, lrecv, at(y, x, 1 - j)) for t in range(nt)]
     def start_all(copies):
         for copy in copies:
             copy.start()
@@ -250,43 +250,24 @@
     for name in ORDER:
         items[name]()
 
-    for copy in gathers + passes + l_copies:
-        copy.wait_send()
-    for m in range(2):
-        for d in range(ny):
-            xt, away, _ = place_copy(m, d)
-
-            @pl.when(xt != x)
-            def _():
-                away().wait_send()
-    for m in range(2, 2 * nt):
-        xt, away, _ = x_copy(m)
-
-        @pl.when(xt != x)
-        def _():
-            away().wait_send()
-    for t in range(1, nt):
-        for p in range(2):
-            for q in range(2):
-                @pl.when(is_holder)
-                def _():
-                    y_copy(t, p, q, s_own, 0, y_outer).wait_send()
-                    y_copy(t, p, q, s_own, 1, y_partner).wait_send()
-
-                @pl.when(jnp.logical_not(is_holder))
-                def _():
-                    y_copy(t, p, q, 1 - s_own, 0, y_next).wait_send()
-    for t in range(nt):
-        for h in range(2):
-            far_copy(t, h).wait_send()
-            end_copy(t, 1 - h, h).wait_send()
-    for t in range(nt - 1):
-        for h in range(2):
-            end_copy(t, h, h).wait_send()
+    landed(l_v.at[pl.ds(0, (nt + 1) * BLOCK // 2), :], lsend)
+    landed(b_v, gsend)
+    landed(b_col.at[pl.ds(0, 2 * (ny - 1))], psem)
+
+    @pl.when(y // 2 == x % 2)
+    def _():
+        landed(b_v.at[:, pl.ds(0, (nt - 1) * BLOCK)], xsend)
+        landed(b_all.at[pl.ds(0, nt - 1)], ysend)
+
+    @pl.when(y // 2 != x % 2)
+    def _():
+        landed(b_v.at[:, pl.ds(0, 2 * (nt - 1) * BLOCK)], xsend)
+        landed(b_all.at[pl.ds(0, nt - 1), :, 0], ysend)
+
+    landed(far_in, fsend)
     for h in range(2):
         finish(nt - 1, h)
-    for h in range(2):
-        end_copy(nt - 1, h, h).wait_send()
+    landed(end_in, esend)
 
 
 def solution(mesh):
@@ -311,8 +292,7 @@
                 pltpu.VMEM((nt, 2, 2, 2, cols, BLOCK), F32),
                 pltpu.VMEM((nt, 2, cols, BLOCK), F32),
                 pltpu.VMEM((nt, 2, 2, cols, BLOCK), F32),
-                dma((nt,)), dma((nt,)), dma((nt,)), dma, dma((6 + 2 * ny,)), dma((2 * ny,)), dma((2 * nt,)),
-                dma((nt, 2, 2, 2)), dma((nt, 2, 2, 2)), dma((nt, 6)), dma((nt, 2)), dma((nt, 2, 2)),
+                *[dma] * 10, dma((2 * ny,)), dma((nt, 2, 2, 2)), dma((nt, 2)), dma((nt, 2)),
             ],
             compiler_params=pltpu.CompilerParams(collective_id=0, has_side_effects=True),
         )(lower_loc, rhs_loc.T).T

time: 37.8 us -> 36.6 us (0.968)
  Pallas kernels: 36.9 us -> 35.7 us
    pallas_call x1, Pallas kernels: 36.9 us -> 35.7 us  [local_product(): pl.pallas_call(functools.partial(kernel, ny, nx, nt), out_shape=pltpu.VME...]
where the time goes in v5:
time: 36.6 us; the launch traced here: 36.4 us
  Pallas kernels  35.7 us (98%)
  local copies, waits for them, and re-layouts  0.72 us (2%)
    pallas_call x1, Pallas kernels, local_product(): pl.pallas_call(functools.partial(kernel, ny, nx, nt), out_shape=pltpu.VME...  35.7 us

profile of v5, /device:TPU:98, one launch (start us, length us, event | category | flops | bytes accessed | tf_op | source)
XLA Modules:
  0.0 36.4 jit_solution(3376574492976830872)
XLA Ops:
  0.0 35.7 %shard_map.28 = bf16[96,1536]{1,0:T(8,128)(2,1)S(1)} custom-call(bf16[1536,768]{1,0:T(8,128)(2,1)} %l_hbm.1, bf16[96,1536]{1,0:T(8,128)(2,1)} %bitcast.3), custom_call_target="tpu_custom_call" | custom-call | tf_op jit(solution)/shard_map/pallas_call | solution.py:282
  35.7 0.7 %copy.4 = bf16[1536,96]{0,1:T(8,128)(2,1)} copy(bf16[1536,96]{0,1:T(8,128)(2,1)S(1)} %bitcast.2) | data formatting | bytes 589824

commit v6 on v5

--- a/solution.py
+++ b/solution.py
@@ -8,8 +8,9 @@
 from jax.sharding import PartitionSpec as P
 
 ORDER = (
-    "g", "p0", "x1", "L", "a01", "a03", "a11", "a13", "x2", "a02", "a12", "h1", "E0", "M0", "h2", "fe1",
-    "fm1", "G0", "E1", "fe2", "M1", "fm2", "E2", "M2", "G1", "F0", "G2", "F1",
+    "g", "x1", "L", "p0", "a01", "a03", "a13", "a11", "x2", "a02", "a12", "he1", "E0", "hm1", "M0", "he2",
+    "fe1", "hm2", "fm1", "Ga0", "Gb0", "E1", "fe2", "M1", "fm2", "E2", "Ga1", "Gb1", "M2", "F0", "Ga2",
+    "Gb2", "F1",
 )
 BLOCK = 256
 CORES = 2
@@ -128,14 +129,13 @@
     def b_came(t, p, s, q):
         landed(b_all.at[t, p, s, q], brecv.at[t, p, s, q])
 
-    def forward_held(t):
+    def forward_held(t, p):
         @pl.when(is_holder)
         def _():
-            for p in (p_end, p_mid):
-                for q in range(2):
-                    b_came(t, p, s_own, q)
-                    y_copy(t, p, s_own, q, y_outer).start()
-                    y_copy(t, p, s_own, q, y_partner).start()
+            for q in range(2):
+                b_came(t, p, s_own, q)
+                y_copy(t, p, s_own, q, y_outer).start()
+                y_copy(t, p, s_own, q, y_partner).start()
 
     def forward_passed(t, p):
         @pl.when(jnp.logical_not(is_holder))
@@ -144,46 +144,56 @@
                 b_came(t, p, 1 - s_own, q)
                 y_copy(t, p, 1 - s_own, q, y_next).start()
 
-    def compute(t, role):
+    def product(p, u, s, m):
+        lhs = b_all[u, p, s].reshape(2 * cols, BLOCK)
+        rhs = l_v[m * BLOCK:(m + 1) * BLOCK, pl.ds(pl.multiple_of((2 * u + s) * BLOCK, BLOCK), BLOCK)]
+        return lax.dot_general(lhs, rhs, (((1,), (1,)), ((), ())), preferred_element_type=F32).reshape(2, cols, BLOCK)
+
+    def await_first(p):
+        for s in range(2):
+            @pl.when(CORES * x + s <= y + ny)
+            def _():
+                for q in range(2):
+                    b_came(0, p, s, q)
+
+    def await_rest(p):
+        for s in range(2):
+            @pl.when(CORES * x + s > y + ny)
+            def _():
+                for q in range(2):
+                    b_came(0, p, s, q)
+
+    def compute(t, role, sends):
         p = (p_end, p_mid)[role]
+        s_last = 1 - s_first
         if t == 0:
-            for s in range(2):
-                @pl.when(CORES * x + s <= y + ny)
-                def _():
-                    for q in range(2):
-                        b_came(t, p, s, q)
-        else:
-            for q in range(2):
-                b_came(t, p, 1 - s_first, q)
+            await_first(p)
         if t == 1:
-            for s in range(2):
-                @pl.when(CORES * x + s > y + ny)
-                def _():
-                    for q in range(2):
-                        b_came(0, p, s, q)
+            await_rest(p)
         if role == 0 and t == 0:
             l_all = l_v.at[pl.ds(0, (nt + 1) * BLOCK // 2), :]
             landed(l_all, l_sem)
             landed(l_all, lrecv)
+        if t:
+            for h in range(2):
+                acc = product(p, t, s_first, 2 * t + h)
+                for u in range(t):
+                    for s in range(2):
+                        acc += product(p, u, s, 2 * t + h)
+                part[t, role, :, h] = acc
+            for q in range(2):
+                b_came(t, p, s_last, q)
         for h in range(2):
             m = 2 * t + h
-            if t == 0:
+            if t:
+                part[t, role, :, h] += product(p, t, s_last, m)
+            else:
                 part[t, role, :, h] = jnp.zeros((2, cols, BLOCK), F32)
                 for s in range(2):
                     @pl.when(CORES * x + s <= y + ny * h)
                     def _():
-                        lhs = b_all[0, p, s].reshape(2 * cols, BLOCK)
-                        rhs = l_v[m * BLOCK:(m + 1) * BLOCK, s * BLOCK:(s + 1) * BLOCK]
-                        acc = lax.dot_general(lhs, rhs, (((1,), (1,)), ((), ())), preferred_element_type=F32)
-                        part[t, role, :, h] += acc.reshape(2, cols, BLOCK)
-                continue
-            acc = jnp.zeros((2 * cols, BLOCK), F32)
-            for u in range(t + 1):
-                for s in range(2):
-                    lhs = b_all[u, p, s].reshape(2 * cols, BLOCK)
-                    rhs = l_v[m * BLOCK:(m + 1) * BLOCK, (2 * u + s) * BLOCK:(2 * u + s + 1) * BLOCK]
-                    acc += lax.dot_general(lhs, rhs, (((1,), (1,)), ((), ())), preferred_element_type=F32)
-            part[t, role, :, h] = acc.reshape(2, cols, BLOCK)
+                        part[t, role, :, h] += product(p, 0, s, m)
+            sends[h].start()
 
     q_own = x // 2
 
@@ -195,20 +205,16 @@
         return remote(part.at[t, 1, xx // 2, h], end_in.at[t, h, side], esend, end_sem.at[t, h], at(y, xx))
 
     def ends(t):
-        compute(t, 0)
-        far_copy(t, 0).start()
-        far_copy(t, 1).start()
+        compute(t, 0, [far_copy(t, 0), far_copy(t, 1)])
 
     def middles(t):
-        compute(t, 1)
-        end_copy(t, 0, 1).start()
-        end_copy(t, 1, 0).start()
-
-    def merge(t):
-        for h, xx in ((0, xr), (1, xl)):
-            landed(far_in.at[t, h], far_sem.at[t, h])
-            part[t, 1, xx // 2, h] += far_in[t, h]
-            end_copy(t, h, h).start()
+        compute(t, 1, [end_copy(t, 1, 0), end_copy(t, 0, 1)])
+
+    def merge(t, h):
+        xx = xl if h else xr
+        landed(far_in.at[t, h], far_sem.at[t, h])
+        part[t, 1, xx // 2, h] += far_in[t, h]
+        end_copy(t, h, h).start()
 
     def finish(t, h):
         landed(end_in.at[t, h], end_sem.at[t, h])
@@ -239,13 +245,15 @@
     }
     for t in range(1, nt):
         items["x%d" % t] = functools.partial(x_first, t)
-        items["h%d" % t] = functools.partial(forward_held, t)
+        items["he%d" % t] = functools.partial(forward_held, t, p_end)
+        items["hm%d" % t] = functools.partial(forward_held, t, p_mid)
         items["fe%d" % t] = functools.partial(forward_passed, t, p_end)
         items["fm%d" % t] = functools.partial(forward_passed, t, p_mid)
     for t in range(nt):
         items["E%d" % t] = functools.partial(ends, t)
         items["M%d" % t] = functools.partial(middles, t)
-        items["G%d" % t] = functools.partial(merge, t)
+        items["Ga%d" % t] = functools.partial(merge, t, 0)
+        items["Gb%d" % t] = functools.partial(merge, t, 1)
         items["F%d" % t] = lambda t=t: [finish(t, h) for h in range(2)]
     for name in ORDER:
         items[name]()

time: 36.6 us -> 36.3 us (level)
  the two profiles are of different devices: /device:TPU:98 before, /device:TPU:96 now
where the time goes in v6:
time: 36.3 us; the launch traced here: 36.2 us
  Pallas kernels  35.4 us (98%)
  local copies, waits for them, and re-layouts  0.72 us (2%)
    pallas_call x1, Pallas kernels, local_product(): pl.pallas_call(functools.partial(kernel, ny, nx, nt), out_shape=pltpu.VME...  35.4 us

profile of v6, /device:TPU:96, one launch (start us, length us, event | category | flops | bytes accessed | tf_op | source)
XLA Modules:
  0.0 36.2 jit_solution(13991036823181988436)
XLA Ops:
  0.0 35.4 %shard_map.28 = bf16[96,1536]{1,0:T(8,128)(2,1)S(1)} custom-call(bf16[1536,768]{1,0:T(8,128)(2,1)} %l_hbm.1, bf16[96,1536]{1,0:T(8,128)(2,1)} %bitcast.3), custom_call_target="tpu_custom_call" | custom-call | tf_op jit(solution)/shard_map/pallas_call | solution.py:290
  35.4 0.7 %copy.4 = bf16[1536,96]{0,1:T(8,128)(2,1)} copy(bf16[1536,96]{0,1:T(8,128)(2,1)S(1)} %bitcast.2) | data formatting | bytes 589824

commit v7 on v6

--- a/solution.py
+++ b/solution.py
@@ -17,8 +17,8 @@
 F32, BF16 = jnp.float32, jnp.bfloat16
 
 
-def kernel(ny, nx, nt, l_hbm, b_hbm, x_out, l_v, b_v, b_col, b_all, part, far_in, end_in, l_sem, lsend, lrecv, bload, gsend, psem,
-           xsend, ysend, fsend, esend, grecv, brecv, far_sem, end_sem):
+def kernel(ny, nx, nt, l_hbm, b_hbm, x_out, l_v, b_v, b_col, b_all, part, far_in, end_in, l_sem, lsend, lrecv, bload, gsend,
+           xsend, ysend, fsend, esend, grecv, bfirst, brecv, far_sem, end_sem):
     cols = b_hbm.shape[0]
     y = lax.axis_index("row")
     c = lax.axis_index("col")
@@ -78,9 +78,9 @@
     def place_copy(m, d):
         yy = (y + d) % ny
         src = b_col.at[ny * m + yy] if d else b_block(m)
-        dst, sem = b_all.at[0, chunk_p, yy % 2, chunk_q], brecv.at[0, chunk_p, yy % 2, chunk_q]
+        dst, sem = b_all.at[0, chunk_p, yy % 2, chunk_q], bfirst.at[chunk_p, yy % 2]
         xt = yy // 2 + 2 * m
-        return xt, (lambda: remote(src, dst, psem, sem, at(y, xt))), (lambda: pltpu.make_async_copy(src, dst, sem))
+        return xt, (lambda: remote(src, dst, gsend, sem, at(y, xt))), (lambda: pltpu.make_async_copy(src, dst, sem))
 
     def came(m, d):
         k = ny * m + (y + d) % ny
@@ -99,7 +99,7 @@
 
     def x_copy(m):
         xt = y // 2 + 2 * (m % 2)
-        dst, sem = b_all.at[m // 2, chunk_p, s_own, chunk_q], brecv.at[m // 2, chunk_p, s_own, chunk_q]
+        dst, sem = b_all.at[m // 2, chunk_p, s_own, chunk_q], brecv.at[m // 2 - 1, chunk_p, s_own, chunk_q]
         return xt, (lambda: remote(b_block(m), dst, xsend, sem, at(y, xt))), (lambda: pltpu.make_async_copy(b_block(m), dst, sem))
 
     def x_first(t):
@@ -124,10 +124,10 @@
 
     def y_copy(t, p, s, q, yy):
         r = b_all.at[t, p, s, q]
-        return remote(r, r, ysend, brecv.at[t, p, s, q], at(yy, x))
+        return remote(r, r, ysend, brecv.at[t - 1, p, s, q], at(yy, x))
 
     def b_came(t, p, s, q):
-        landed(b_all.at[t, p, s, q], brecv.at[t, p, s, q])
+        landed(b_all.at[t, p, s, q], brecv.at[t - 1, p, s, q])
 
     def forward_held(t, p):
         @pl.when(is_holder)
@@ -153,15 +153,13 @@
         for s in range(2):
             @pl.when(CORES * x + s <= y + ny)
             def _():
-                for q in range(2):
-                    b_came(0, p, s, q)
+                landed(b_all.at[0, p, s], bfirst.at[p, s])
 
     def await_rest(p):
         for s in range(2):
             @pl.when(CORES * x + s > y + ny)
             def _():
-                for q in range(2):
-                    b_came(0, p, s, q)
+                landed(b_all.at[0, p, s], bfirst.at[p, s])
 
     def compute(t, role, sends):
         p = (p_end, p_mid)[role]
@@ -259,8 +257,7 @@
         items[name]()
 
     landed(l_v.at[pl.ds(0, (nt + 1) * BLOCK // 2), :], lsend)
-    landed(b_v, gsend)
-    landed(b_col.at[pl.ds(0, 2 * (ny - 1))], psem)
+    landed(b_all.at[:, :, 0], gsend)
 
     @pl.when(y // 2 == x % 2)
     def _():
@@ -300,7 +297,7 @@
                 pltpu.VMEM((nt, 2, 2, 2, cols, BLOCK), F32),
                 pltpu.VMEM((nt, 2, cols, BLOCK), F32),
                 pltpu.VMEM((nt, 2, 2, cols, BLOCK), F32),
-                *[dma] * 10, dma((2 * ny,)), dma((nt, 2, 2, 2)), dma((nt, 2)), dma((nt, 2)),
+                *[dma] * 9, dma((2 * ny,)), dma((2, 2)), dma((nt - 1, 2, 2, 2)), dma((nt, 2)), dma((nt, 2)),
             ],
             compiler_params=pltpu.CompilerParams(collective_id=0, has_side_effects=True),
         )(lower_loc, rhs_loc.T).T

time: 36.3 us -> 36.2 us (level)
  no operation moved by 1% of the time
where the time goes in v7:
time: 36.2 us; the launch traced here: 36.1 us
  Pallas kernels  35.4 us (98%)
  local copies, waits for them, and re-layouts  0.72 us (2%)
    pallas_call x1, Pallas kernels, local_product(): pl.pallas_call(functools.partial(kernel, ny, nx, nt), out_shape=pltpu.VME...  35.4 us

profile of v7, /device:TPU:96, one launch (start us, length us, event | category | flops | bytes accessed | tf_op | source)
XLA Modules:
  0.0 36.1 jit_solution(12859976892647909725)
XLA Ops:
  0.0 35.4 %shard_map.28 = bf16[96,1536]{1,0:T(8,128)(2,1)S(1)} custom-call(bf16[1536,768]{1,0:T(8,128)(2,1)} %l_hbm.1, bf16[96,1536]{1,0:T(8,128)(2,1)} %bitcast.3), custom_call_target="tpu_custom_call" | custom-call | tf_op jit(solution)/shard_map/pallas_call | solution.py:287
  35.4 0.7 %copy.4 = bf16[1536,96]{0,1:T(8,128)(2,1)} copy(bf16[1536,96]{0,1:T(8,128)(2,1)S(1)} %bitcast.2) | data formatting | bytes 589824

commit v8 on v7

--- a/solution.py
+++ b/solution.py
@@ -17,7 +17,7 @@
 F32, BF16 = jnp.float32, jnp.bfloat16
 
 
-def kernel(ny, nx, nt, l_hbm, b_hbm, x_out, l_v, b_v, b_col, b_all, part, far_in, end_in, l_sem, lsend, lrecv, bload, gsend,
+def kernel(ny, nx, nt, l_hbm, b_hbm, x_out, l_v, b_v, b_col, b_all, part, far_in, end_in, l_sem, lsend, bload, gsend,
            xsend, ysend, fsend, esend, grecv, bfirst, brecv, far_sem, end_sem):
     cols = b_hbm.shape[0]
     y = lax.axis_index("row")
@@ -169,9 +169,7 @@
         if t == 1:
             await_rest(p)
         if role == 0 and t == 0:
-            l_all = l_v.at[pl.ds(0, (nt + 1) * BLOCK // 2), :]
-            landed(l_all, l_sem)
-            landed(l_all, lrecv)
+            landed(l_v.at[pl.ds(0, (nt + 1) * BLOCK), :], l_sem)
         if t:
             for h in range(2):
                 acc = product(p, t, s_first, 2 * t + h)
@@ -219,7 +217,7 @@
         m = 2 * t + h
         x_out[:, m * BLOCK:(m + 1) * BLOCK] = (part[t, 0, q_own, h] + (end_in[t, h, 0] + end_in[t, h, 1])).astype(BF16)
 
-    l_copies = [remote(l_src(t), l_v.at[l_slice(t, j)], lsend, lrecv, at(y, x, 1 - j)) for t in range(nt)]
+    l_copies = [remote(l_src(t), l_v.at[l_slice(t, j)], lsend, l_sem, at(y, x, 1 - j)) for t in range(nt)]
     def start_all(copies):
         for copy in copies:
             copy.start()
@@ -297,7 +295,7 @@
                 pltpu.VMEM((nt, 2, 2, 2, cols, BLOCK), F32),
                 pltpu.VMEM((nt, 2, cols, BLOCK), F32),
                 pltpu.VMEM((nt, 2, 2, cols, BLOCK), F32),
-                *[dma] * 9, dma((2 * ny,)), dma((2, 2)), dma((nt - 1, 2, 2, 2)), dma((nt, 2)), dma((nt, 2)),
+                *[dma] * 8, dma((2 * ny,)), dma((2, 2)), dma((nt - 1, 2, 2, 2)), dma((nt, 2)), dma((nt, 2)),
             ],
             compiler_params=pltpu.CompilerParams(collective_id=0, has_side_effects=True),
         )(lower_loc, rhs_loc.T).T

time: 36.2 us -> 36.2 us (level)
  no operation moved by 1% of the time
where the time goes in v8:
time: 36.2 us; the launch traced here: 36.1 us
  Pallas kernels  35.4 us (98%)
  local copies, waits for them, and re-layouts  0.72 us (2%)
    pallas_call x1, Pallas kernels, local_product(): pl.pallas_call(functools.partial(kernel, ny, nx, nt), out_shape=pltpu.VME...  35.4 us

profile of v8, /device:TPU:96, one launch (start us, length us, event | category | flops | bytes accessed | tf_op | source)
XLA Modules:
  0.0 36.1 jit_solution(1055054697736931818)
XLA Ops:
  0.0 35.4 %shard_map.28 = bf16[96,1536]{1,0:T(8,128)(2,1)S(1)} custom-call(bf16[1536,768]{1,0:T(8,128)(2,1)} %l_hbm.1, bf16[96,1536]{1,0:T(8,128)(2,1)} %bitcast.3), custom_call_target="tpu_custom_call" | custom-call | tf_op jit(solution)/shard_map/pallas_call | solution.py:285
  35.4 0.7 %copy.4 = bf16[1536,96]{0,1:T(8,128)(2,1)} copy(bf16[1536,96]{0,1:T(8,128)(2,1)S(1)} %bitcast.2) | data formatting | bytes 589824
